TPU v7x, 64 devices: a 2x2x8 block of a 4x4x8 slice. The times are simulated.
64 devices in a mesh: dp: 8 (over x, y, core), tp: 8 (over z).
Axes of the slice: x: 2, y: 2, z: 8, core: 2. Of those that a mesh axis runs over, the one named last changes fastest.
The devices are a block of a 4x4x8 slice.
Arguments:
- x: bfloat16 [1024, 7168], P('dp'), parts along dimension 0
- w_gate: bfloat16 [7168, 20480], P(None, 'tp')
- w_up: bfloat16 [7168, 20480], P(None, 'tp')
- w_down: bfloat16 [20480, 7168], P('tp')
Outputs:
- output: bfloat16 [1024, 7168], P('dp'), parts along dimension 0
There are 8 independent parts. A program takes and returns all parts, laid end to end along the dimension named above; an argument that names none is the same for every part.
All inputs are finite; a program needn't handle non-finite values.
Results may differ from a plain program's by a relative error of at most 0.016.
Values are sent between devices in bfloat16 or wider.
A program may use at most 768 MiB of HBM per device.

v0:
```python
import jax
import jax.numpy as jnp
from jax import lax
from jax.sharding import PartitionSpec as P


def solution(mesh):
    def step(x, w_gate, w_up, w_down):
        gate = jnp.dot(x, w_gate, preferred_element_type=jnp.float32)
        up = jnp.dot(x, w_up, preferred_element_type=jnp.float32)
        hidden = (jax.nn.silu(gate) * up).astype(jnp.bfloat16)
        term = jnp.dot(hidden, w_down, preferred_element_type=jnp.float32).astype(jnp.bfloat16)
        return lax.psum(term, "tp")

    return jax.shard_map(
        step,
        mesh=mesh,
        in_specs=(P("dp", None), P(None, "tp"), P(None, "tp"), P("tp", None)),
        out_specs=P("dp", None),
        check_vma=False,
    )
```

profile of v0, /device:TPU:22, one launch (start us, length us, event | category | flops | bytes accessed | tf_op | source)
XLA Modules:
  0.0 135.9 jit_solution(3609077118539958308)
XLA Ops:
  6.5 0.0 copy-start
  6.6 0.0 all-reduce.2.cloned.1.call-start
  6.6 1.5 %copy-done = bf16[128,7168]{1,0:T(8,128)(2,1)S(1)} copy-done((bf16[128,7168]{1,0:T(8,128)(2,1)S(1)}, bf16[128,7168]{1,0:T(8,128)(2,1)}, u32[]{:S(2)}) %copy-start) | copy-done | bytes 1835032
  8.1 14.0 %fusion.2 = f32[128,2560]{1,0:T(8,128)S(1)} fusion(bf16[128,7168]{1,0:T(8,128)(2,1)S(1)} %copy-done, bf16[7168,2560]{1,0:T(8,128)(2,1)} %param.5), kind=kOutput, calls=%fused_computation.4 | convolution fusion | flops 4697620480 | bytes 39845888 | tf_op jit(solution)/shard_map/dot_general | solution.py:9
  22.1 26.7 %convolution_convert_fusion = bf16[128,7168]{1,0:T(8,128)(2,1)} fusion(bf16[2560,7168]{1,0:T(8,128)(2,1)} %param.7, bf16[128,7168]{1,0:T(8,128)(2,1)S(1)} %copy-done, bf16[7168,2560]{1,0:T(8,128)(2,1)} %param.6, f32[128,2560]{1,0:T(8,128)S(1)} %fusion.2), kind=kOutput, calls=%fused_computation | convolution fusion | flops 9398124544 | bytes 78381056 | tf_op jit(solution)/shard_map/dot_general | solution.py:12
  48.8 0.1 all-reduce.2.cloned.1.call-update
  48.9 0.0 copy-start.1
  48.9 77.3 %all-reduce.2.cloned.1.call-done = bf16[128,7168]{1,0:T(8,128)(2,1)} async-done(((bf16[128,7168]{1,0:T(8,128)(2,1)}), bf16[128,7168]{1,0:T(8,128)(2,1)}) %all-reduce.2.cloned.1.call-update) | async-done | bytes 1835024 | tf_op jit(solution)/shard_map/psum | solution.py:13
  126.2 2.8 %copy.6 = bf16[128,7168]{1,0:T(8,128)(2,1)} copy(bf16[128,7168]{1,0:T(8,128)(2,1)} %all-reduce.2.cloned.1.call-done) | data formatting | bytes 3670016
  129.0 0.0 copy-done.1
Async XLA Ops:
  6.5 1.5 %copy-start = (bf16[128,7168]{1,0:T(8,128)(2,1)S(1)}, bf16[128,7168]{1,0:T(8,128)(2,1)}, u32[]{:S(2)}) copy-start(bf16[128,7168]{1,0:T(8,128)(2,1)} %param.4) | copy-start | bytes 5505028
  6.6 119.6 %all-reduce.2.cloned.1.call-start = ((), (), s32[]{:S(2)}) async-start(), calls=%async_computation | async-start | bytes 3670016 | tf_op jit(solution)/shard_map/psum | solution.py:13
  48.9 80.2 %copy-start.1 = (bf16[128,7168]{1,0:T(8,128)(2,1)S(1)}, bf16[128,7168]{1,0:T(8,128)(2,1)}, u32[]{:S(2)}) copy-start(bf16[128,7168]{1,0:T(8,128)(2,1)} %param.4) | copy-start | bytes 5505028
Sparse Core Ops, SparseCore 0:
  49.0 77.1 all-reduce.1
where the time goes:
time: 136 us
  waiting for transfers between devices  77.4 us (57%)
  matrix products  40.8 us (30%)
  between operations  13.4 us (10%)
  local copies, waits for them, and re-layouts  4.35 us (3%)
    psum x1, waiting for transfers between devices, step(): return lax.psum(term, 'tp')  77.3 us
    dot_general x1, matrix products, step(): jnp.dot(hidden, w_down, preferred_element_type=jnp.float32)  26.7 us
    dot_general x1, matrix products, step(): gate = jnp.dot(x, w_gate, preferred_element_type=jnp.float32)  14 us
    unnamed x5, local copies, waits for them, and re-layouts  4.35 us
  transfers between devices with their start and end apart: 1, of which 1 were waited for; matrix products, arithmetic and copies ran while one was open for 0% of the time, Pallas kernels for 0%

commit v1 on v0

v1 whole, which is shorter than its diff:
```python
import functools

import jax
import jax.numpy as jnp
from jax import lax
from jax.experimental import pallas as pl
from jax.experimental.pallas import tpu as pltpu
from jax.sharding import PartitionSpec as P

MESH = pl.DeviceIdType.MESH
F32, BF16 = jnp.float32, jnp.bfloat16

BLOCK = 256
HALVES = 2
SLOTS = 4
DOWN_SLOTS = 4
PIECES = 4

FIRST = ((0, 1), (2, 3))
SECOND = ((2, 3, 0, 1), (0, 1, 2, 3))
LATER = ((2, 0, 3, 1), (0, 2, 1, 3))
FINAL = (0, 2, 1, 3)
LAST = ((0, 1), (2, 3))


def reduce_plan(hops):
    plans = []
    for way in range(2):
        plan = [(1, r) for r in FIRST[way]] + [(2, r) for r in SECOND[way]]
        for hop in range(3, hops + 1):
            plan += [(hop, r) for r in LATER[way]]
        plans.append(plan)
    return plans


def gather_plan(hops):
    plans = []
    for way in range(2):
        plan = [(hop, r) for hop in range(1, hops) for r in FINAL]
        plans.append(plan + [(hops, r) for r in LAST[way]])
    return plans


def kernel(
    n, x_ref, wg_ref, wu_ref, wd_ref, y_ref,
    xs, gbuf, ubuf, acc_g, acc_u, hid, hout, dbuf, part, rs_out, rs_in,
    x_sem, xr_send, xr_recv, w_sem, h_send, h_recv, d_sem,
    rs_send, rs_recv, ag_send, ag_recv,
):
    rows, depth = x_ref.shape
    cols = wg_ref.shape[1]
    mine = cols // 2
    blocks = mine // BLOCK
    kd = depth // HALVES
    steps = blocks * HALVES
    chunk = depth // n
    hops = n // 2
    height = rows // PIECES

    tp = lax.axis_index("tp")
    dp = lax.axis_index("dp")
    core = lax.rem(dp, 2)
    partner = {"dp": dp + 1 - 2 * core}
    ways = ({"tp": lax.rem(tp + 1, n)}, {"tp": lax.rem(tp + n - 1, n)})
    my_cols = core * mine
    other_cols = mine - my_cols

    def x_copy(h):
        ks = pl.ds(h * kd, kd)
        return pltpu.make_async_copy(x_ref.at[:, ks], xs.at[pl.ds(0, rows), ks], x_sem.at[h])

    def x_remote(h):
        ks = pl.ds(h * kd, kd)
        return pltpu.make_async_remote_copy(
            src_ref=x_ref.at[:, ks], dst_ref=xs.at[pl.ds(rows, rows), ks],
            send_sem=xr_send.at[h], recv_sem=xr_recv.at[h], device_id=partner, device_id_type=MESH,
        )

    def w_copies(step):
        b, h, slot = step // HALVES, step % HALVES, step % SLOTS
        ks = pl.ds(pl.multiple_of(h * kd, kd), kd)
        ns = pl.ds(pl.multiple_of(my_cols + b * BLOCK, BLOCK), BLOCK)
        return (
            pltpu.make_async_copy(wg_ref.at[ks, ns], gbuf.at[slot], w_sem.at[0, slot]),
            pltpu.make_async_copy(wu_ref.at[ks, ns], ubuf.at[slot], w_sem.at[1, slot]),
        )

    def w_start(step):
        for c in w_copies(step):
            c.start()

    def w_wait(step):
        for c in w_copies(step):
            c.wait()

    def chunk_at(k):
        offset = hops if k == 0 else (n if k == n - 1 else (hops - (k + 1) // 2 if k % 2 else n - hops + k // 2))
        return lax.rem(tp + offset, n)

    def columns(c):
        return pl.ds(pl.multiple_of(c * chunk, chunk), chunk)

    def d_copies(k):
        cs = columns(chunk_at(k))
        slot = k % DOWN_SLOTS
        return [
            pltpu.make_async_copy(
                wd_ref.at[pl.ds(pl.multiple_of(o, mine), mine), cs],
                dbuf.at[slot, pl.ds(i * mine, mine)], d_sem.at[slot, i],
            )
            for i, o in enumerate((my_cols, other_cols))
        ]

    def h_copy(b):
        where = pl.ds(pl.multiple_of(mine + b * BLOCK, BLOCK), BLOCK)
        return pltpu.make_async_remote_copy(
            src_ref=hout.at[b], dst_ref=hid.at[:, where],
            send_sem=h_send.at[b], recv_sem=h_recv.at[b], device_id=partner, device_id_type=MESH,
        )

    x_copy(0).start()
    w_start(0)
    x_copy(1).start()
    for s in range(1, SLOTS):
        w_start(s)

    barrier = pltpu.get_barrier_semaphore()
    for who in (partner,) + ways:
        pl.semaphore_signal(barrier, inc=1, device_id=who, device_id_type=MESH)
    pl.semaphore_wait(barrier, 3)
    for h in range(HALVES):
        x_remote(h).start()

    def dot(a, b):
        return jnp.dot(a, b, preferred_element_type=F32)

    def finish(b, gate, up, half):
        hidden = (jax.nn.silu(gate) * up).astype(BF16)
        if half != 1:
            hid[:, pl.ds(pl.multiple_of(b * BLOCK, BLOCK), BLOCK)] = hidden[:rows]
        if half != 0:
            hout[b] = hidden[-rows:]
            h_copy(b).start()

    def half_step(b, h, half):
        rs = pl.ds(half * rows, rows)
        lhs = xs[rs, pl.ds(h * kd, kd)]
        gate, up = dot(lhs, gbuf[h]), dot(lhs, ubuf[h])
        if h == 0:
            acc_g[rs] = gate
            acc_u[rs] = up
        else:
            finish(b, acc_g[rs] + gate, acc_u[rs] + up, half)

    for half in range(2):
        for h in range(HALVES):
            if half == 0:
                x_copy(h).wait()
                w_wait(h)
            else:
                x_remote(h).wait_recv()
            half_step(0, h, half)
            if half == 1:
                w_start(h + SLOTS)

    @pl.loop(1, blocks)
    def _(b):
        for h in range(HALVES):
            step = b * HALVES + h
            slot = lax.rem(step, SLOTS)
            w_wait(step)
            lhs = xs[:, pl.ds(h * kd, kd)]
            gate, up = dot(lhs, gbuf[slot]), dot(lhs, ubuf[slot])
            if h == 0:
                acc_g[...] = gate
                acc_u[...] = up
            else:
                finish(b, acc_g[...] + gate, acc_u[...] + up, 2)

            @pl.when(step + SLOTS < steps)
            def _():
                w_start(step + SLOTS)

            for k in range(DOWN_SLOTS):
                @pl.when(step + SLOTS == steps + k)
                def _():
                    for c in d_copies(k):
                        c.start()

    def compute(k):
        slot = k % DOWN_SLOTS
        for i, c in enumerate(d_copies(k)):
            c.wait()
            if k == 0:
                ks = pl.ds(i * mine, mine)
                if i == 1:
                    for b in range(blocks):
                        h_copy(b).wait_recv()
                p = dot(hid[:, ks], dbuf[slot, ks])
                part[k] = p if i == 0 else part[k] + p
        if k > 0:
            part[k] = dot(hid[...], dbuf[slot])
        if k + DOWN_SLOTS < n:
            for c in d_copies(k + DOWN_SLOTS):
                c.start()

    plan = reduce_plan(hops)
    place = [{m: q for q, m in enumerate(p)} for p in plan]

    def rs_copy(way, q):
        return pltpu.make_async_remote_copy(
            src_ref=rs_out.at[way, q], dst_ref=rs_in.at[way, q],
            send_sem=rs_send.at[way, q], recv_sem=rs_recv.at[way, q],
            device_id=ways[way], device_id_type=MESH,
        )

    def place_of(way, hop):
        return 0 if hop == 1 else 2 * (hop - 1) - 1 + way

    def reduce_send(way, hop, r):
        q = place[way][hop, r]
        term = part[place_of(way, hop), pl.ds(r * height, height)]
        before = place[way].get((hop - 1, r))
        if before is not None:
            rs_copy(way, before).wait_recv()
            term = term + rs_in[way, before].astype(F32)
        rs_out[way, q] = term.astype(BF16)
        rs_copy(way, q).start()

    def reduce_hop(hop, picked):
        for i in picked:
            for way in range(2):
                order = [r for (h, r) in plan[way] if h == hop]
                reduce_send(way, hop, order[i])

    compute(0)
    reduce_hop(1, range(PIECES // 2))
    compute(1)
    for r in SECOND[0][: PIECES // 2]:
        reduce_send(0, 2, r)
    compute(2)
    for r in SECOND[1][: PIECES // 2]:
        reduce_send(1, 2, r)
    for k in range(3, min(5, n)):
        compute(k)
    reduce_hop(2, range(PIECES // 2, PIECES))
    for k in range(5, n - 1):
        compute(k)
    if hops > 2:
        reduce_hop(3, range(PIECES))
    compute(n - 1)
    for hop in range(4, hops + 1):
        reduce_hop(hop, range(PIECES))

    gplan = gather_plan(hops)
    gplace = [{m: q for q, m in enumerate(p)} for p in gplan]

    def ag_copy(way, hop, r):
        q = gplace[way][hop, r]
        back = hop - 1
        owner = lax.rem(tp + (n - back if way == 0 else back), n)
        where = y_ref.at[pl.ds(r * height, height), columns(owner)]
        return pltpu.make_async_remote_copy(
            src_ref=where, dst_ref=where, send_sem=ag_send.at[way, q], recv_sem=ag_recv.at[way, q],
            device_id=ways[way], device_id_type=MESH,
        )

    def ag_arrival(way, hop, r):
        q = gplace[way][hop, r]
        owner = lax.rem(tp + (n - hop if way == 0 else hop), n)
        where = y_ref.at[pl.ds(r * height, height), columns(owner)]
        return pltpu.make_async_remote_copy(
            src_ref=where, dst_ref=where, send_sem=ag_send.at[way, q], recv_sem=ag_recv.at[way, q],
            device_id=ways[way], device_id_type=MESH,
        )

    own = columns(tp)
    for r in FINAL:
        rs = pl.ds(r * height, height)
        total = part[n - 1, rs]
        for way in range(2):
            q = place[way][hops, r]
            rs_copy(way, q).wait_recv()
            total = total + rs_in[way, q].astype(F32)
        y_ref[rs, own] = total.astype(BF16)
        for way in range(2):
            ag_copy(way, 1, r).start()
    for hop in range(1, hops + 1):
        for r in FINAL:
            for way in range(2):
                if (hop, r) in gplace[way]:
                    ag_arrival(way, hop, r).wait_recv()
                    if (hop + 1, r) in gplace[way]:
                        ag_copy(way, hop + 1, r).start()

    for h in range(HALVES):
        x_remote(h).wait_send()
    for b in range(blocks):
        h_copy(b).wait_send()
    for way in range(2):
        for q in range(len(plan[way])):
            rs_copy(way, q).wait_send()
        for hop, r in gplan[way]:
            ag_copy(way, hop, r).wait_send()


def solution(mesh):
    n = mesh.shape["tp"]

    def step(x, w_gate, w_up, w_down):
        rows, depth = x.shape
        cols = w_gate.shape[1]
        mine = cols // 2
        blocks = mine // BLOCK
        kd = depth // HALVES
        chunk = depth // n
        height = rows // PIECES
        messages = len(reduce_plan(n // 2)[0])
        hbm = pl.BlockSpec(memory_space=pltpu.HBM)
        dma = pltpu.SemaphoreType.DMA
        return pl.pallas_call(
            functools.partial(kernel, n),
            out_shape=jax.ShapeDtypeStruct((rows, depth), BF16),
            in_specs=[hbm] * 4,
            out_specs=pl.BlockSpec(memory_space=pltpu.VMEM),
            scratch_shapes=[
                pltpu.VMEM((2 * rows, depth), BF16),
                pltpu.VMEM((SLOTS, kd, BLOCK), BF16),
                pltpu.VMEM((SLOTS, kd, BLOCK), BF16),
                pltpu.VMEM((2 * rows, BLOCK), F32),
                pltpu.VMEM((2 * rows, BLOCK), F32),
                pltpu.VMEM((rows, cols), BF16),
                pltpu.VMEM((blocks, rows, BLOCK), BF16),
                pltpu.VMEM((DOWN_SLOTS, cols, chunk), BF16),
                pltpu.VMEM((n, rows, chunk), F32),
                pltpu.VMEM((2, messages, height, chunk), BF16),
                pltpu.VMEM((2, messages, height, chunk), BF16),
                dma((HALVES,)), dma((HALVES,)), dma((HALVES,)),
                dma((2, SLOTS)), dma((blocks,)), dma((blocks,)),
                dma((DOWN_SLOTS, 2)),
                dma((2, messages)), dma((2, messages)), dma((2, messages)), dma((2, messages)),
            ],
            compiler_params=pltpu.CompilerParams(
                collective_id=0, has_side_effects=True, vmem_limit_bytes=64 * 1024 * 1024 - 65536,
            ),
        )(x, w_gate, w_up, w_down)

    return jax.shard_map(
        step,
        mesh=mesh,
        in_specs=(P("dp", None), P(None, "tp"), P(None, "tp"), P("tp", None)),
        out_specs=P("dp", None),
        check_vma=False,
    )
```

time: 136 us -> 67.6 us (0.50)
  waiting for transfers between devices: 77.4 us -> 0 us
  Pallas kernels: 0 us -> 64.6 us
  matrix products: 40.8 us -> 0 us
  between operations: 13.4 us -> 0.01 us
  local copies, waits for them, and re-layouts: 4.35 us -> 2.85 us
    psum x1 -> x0, waiting for transfers between devices: 77.3 us -> none  [step(): return lax.psum(term, 'tp')]
    pallas_call x0 -> x1, Pallas kernels: none -> 64.6 us  [step(): pl.pallas_call(functools.partial(kernel, n), out_shape=jax.ShapeDtypeStru...]
    dot_general x2 -> x0, matrix products: 40.8 us -> none  [the longest x1 26.7 us: step(): jnp.dot(hidden, w_down, preferred_element_type=jnp.float32)]
    unnamed x5 -> x1, local copies, waits for them, and re-layouts: 4.35 us -> 2.85 us
  transfers between devices with their start and end apart: 1 -> 0, of which waited for: 1 -> 0; matrix products, arithmetic and copies ran while one was open for 0% -> 0% of each run, Pallas kernels for 0% -> 0%
where the time goes in v1:
time: 67.6 us; the launch traced here: 67.4 us
  Pallas kernels  64.6 us (96%)
  local copies, waits for them, and re-layouts  2.85 us (4%)
    pallas_call x1, Pallas kernels, step(): pl.pallas_call(functools.partial(kernel, n), out_shape=jax.ShapeDtypeStru...  64.6 us
    unnamed x1, local copies, waits for them, and re-layouts  2.85 us

profile of v1, /device:TPU:22, one launch (start us, length us, event | category | flops | bytes accessed | tf_op | source)
XLA Modules:
  0.0 67.4 jit_solution(9314362282626959245)
XLA Ops:
  0.0 64.6 %shard_map.46 = bf16[128,7168]{1,0:T(8,128)(2,1)} custom-call(bf16[128,7168]{1,0:T(8,128)(2,1)} %x_ref.1, bf16[7168,2560]{1,0:T(8,128)(2,1)} %wg_ref.1, bf16[7168,2560]{1,0:T(8,128)(2,1)} %wu_ref.1, bf16[2560,7168]{1,0:T(8,128)(2,1)} %wd_ref.1), custom_call_target="tpu_custom_call" | custom-call | tf_op jit(solution)/shard_map/pallas_call | solution.py:321
  64.6 2.8 %copy.6 = bf16[128,7168]{1,0:T(8,128)(2,1)} copy(bf16[128,7168]{1,0:T(8,128)(2,1)} %shard_map.46) | data formatting | bytes 3670016

commit v2 on v1

--- a/solution.py
+++ b/solution.py
@@ -10,17 +10,25 @@
 MESH = pl.DeviceIdType.MESH
 F32, BF16 = jnp.float32, jnp.bfloat16
 
-BLOCK = 256
-HALVES = 2
-SLOTS = 4
+TILE = 256
+PARTS = 4
+SLOTS = 12
+AHEAD = 3
 DOWN_SLOTS = 4
 PIECES = 4
 
-FIRST = ((0, 1), (2, 3))
-SECOND = ((2, 3, 0, 1), (0, 1, 2, 3))
-LATER = ((2, 0, 3, 1), (0, 2, 1, 3))
-FINAL = (0, 2, 1, 3)
-LAST = ((0, 1), (2, 3))
+LOWER, UPPER = tuple(range(PIECES // 2)), tuple(range(PIECES // 2, PIECES))
+
+
+def mixed(a, b):
+    return tuple(r for pair in zip(a, b) for r in pair)
+
+
+FIRST = (LOWER, UPPER)
+SECOND = (UPPER + LOWER, LOWER + UPPER)
+LATER = (mixed(UPPER, LOWER), mixed(LOWER, UPPER))
+FINAL = mixed(LOWER, UPPER)
+LAST = (LOWER, UPPER)
 
 
 def reduce_plan(hops):
@@ -43,16 +51,17 @@
 
 def kernel(
     n, x_ref, wg_ref, wu_ref, wd_ref, y_ref,
-    xs, gbuf, ubuf, acc_g, acc_u, hid, hout, dbuf, part, rs_out, rs_in,
+    xs, gbuf, ubuf, gacc, uacc, hid, hout, dbuf, part, rs_out, rs_in,
     x_sem, xr_send, xr_recv, w_sem, h_send, h_recv, d_sem,
     rs_send, rs_recv, ag_send, ag_recv,
 ):
     rows, depth = x_ref.shape
     cols = wg_ref.shape[1]
     mine = cols // 2
-    blocks = mine // BLOCK
-    kd = depth // HALVES
-    steps = blocks * HALVES
+    blocks = mine // TILE
+    kd = depth // PARTS
+    tiles = kd // TILE
+    steps = blocks * PARTS
     chunk = depth // n
     hops = n // 2
     height = rows // PIECES
@@ -72,27 +81,19 @@
     def x_remote(h):
         ks = pl.ds(h * kd, kd)
         return pltpu.make_async_remote_copy(
-            src_ref=x_ref.at[:, ks], dst_ref=xs.at[pl.ds(rows, rows), ks],
+            src_ref=xs.at[pl.ds(0, rows), ks], dst_ref=xs.at[pl.ds(rows, rows), ks],
             send_sem=xr_send.at[h], recv_sem=xr_recv.at[h], device_id=partner, device_id_type=MESH,
         )
 
     def w_copies(step):
-        b, h, slot = step // HALVES, step % HALVES, step % SLOTS
-        ks = pl.ds(pl.multiple_of(h * kd, kd), kd)
-        ns = pl.ds(pl.multiple_of(my_cols + b * BLOCK, BLOCK), BLOCK)
+        b, h, slot = step // PARTS, step % PARTS, step % SLOTS
+        ks = pl.ds(h * kd, kd)
+        ns = pl.ds(pl.multiple_of(my_cols + b * TILE, TILE), TILE)
         return (
             pltpu.make_async_copy(wg_ref.at[ks, ns], gbuf.at[slot], w_sem.at[0, slot]),
             pltpu.make_async_copy(wu_ref.at[ks, ns], ubuf.at[slot], w_sem.at[1, slot]),
         )
 
-    def w_start(step):
-        for c in w_copies(step):
-            c.start()
-
-    def w_wait(step):
-        for c in w_copies(step):
-            c.wait()
-
     def chunk_at(k):
         offset = hops if k == 0 else (n if k == n - 1 else (hops - (k + 1) // 2 if k % 2 else n - hops + k // 2))
         return lax.rem(tp + offset, n)
@@ -100,109 +101,111 @@
     def columns(c):
         return pl.ds(pl.multiple_of(c * chunk, chunk), chunk)
 
-    def d_copies(k):
-        cs = columns(chunk_at(k))
+    def d_copy(k, i):
         slot = k % DOWN_SLOTS
-        return [
-            pltpu.make_async_copy(
-                wd_ref.at[pl.ds(pl.multiple_of(o, mine), mine), cs],
-                dbuf.at[slot, pl.ds(i * mine, mine)], d_sem.at[slot, i],
-            )
-            for i, o in enumerate((my_cols, other_cols))
-        ]
+        o = (my_cols, other_cols)[i]
+        return pltpu.make_async_copy(
+            wd_ref.at[pl.ds(pl.multiple_of(o, mine), mine), columns(chunk_at(k))],
+            dbuf.at[slot, pl.ds(i * mine, mine)], d_sem.at[slot, i],
+        )
 
     def h_copy(b):
-        where = pl.ds(pl.multiple_of(mine + b * BLOCK, BLOCK), BLOCK)
-        return pltpu.make_async_remote_copy(
-            src_ref=hout.at[b], dst_ref=hid.at[:, where],
+        return pltpu.make_async_remote_copy(
+            src_ref=hout.at[b], dst_ref=hid.at[:, pl.ds(mine + b * TILE, TILE)],
             send_sem=h_send.at[b], recv_sem=h_recv.at[b], device_id=partner, device_id_type=MESH,
         )
 
-    x_copy(0).start()
-    w_start(0)
-    x_copy(1).start()
-    for s in range(1, SLOTS):
-        w_start(s)
+    loads = [w_copies(s) for s in range(steps)] + [
+        (d_copy(k, i),) for k in range(DOWN_SLOTS) for i in range(2)
+    ]
+
+    def start_load(j):
+        if j < len(loads):
+            for c in loads[j]:
+                c.start()
+
+    for h in range(PARTS):
+        x_copy(h).start()
+    for j in range(AHEAD):
+        start_load(j)
 
     barrier = pltpu.get_barrier_semaphore()
     for who in (partner,) + ways:
         pl.semaphore_signal(barrier, inc=1, device_id=who, device_id_type=MESH)
+
     pl.semaphore_wait(barrier, 3)
-    for h in range(HALVES):
+    for h in range(PARTS):
+        x_copy(h).wait()
         x_remote(h).start()
 
     def dot(a, b):
         return jnp.dot(a, b, preferred_element_type=F32)
 
-    def finish(b, gate, up, half):
-        hidden = (jax.nn.silu(gate) * up).astype(BF16)
-        if half != 1:
-            hid[:, pl.ds(pl.multiple_of(b * BLOCK, BLOCK), BLOCK)] = hidden[:rows]
-        if half != 0:
-            hout[b] = hidden[-rows:]
-            h_copy(b).start()
-
-    def half_step(b, h, half):
+    def arrive(b, h):
+        for c in w_copies(b * PARTS + h):
+            c.wait()
+
+    def multiply(b, first, count, at, size):
+        rs = pl.ds(at, size)
+        lhs = xs[rs, pl.ds(first * kd, count * kd)]
+        slot = (b * PARTS + first) % SLOTS
+        for buf, acc in ((gbuf, gacc), (ubuf, uacc)):
+            product = dot(lhs, buf[pl.ds(slot, count)].reshape(count * kd, TILE))
+            acc[b % 2, rs] = product if first == 0 else acc[b % 2, rs] + product
+
+    def hidden(b, half):
         rs = pl.ds(half * rows, rows)
-        lhs = xs[rs, pl.ds(h * kd, kd)]
-        gate, up = dot(lhs, gbuf[h]), dot(lhs, ubuf[h])
-        if h == 0:
-            acc_g[rs] = gate
-            acc_u[rs] = up
+        value = (jax.nn.silu(gacc[b % 2, rs]) * uacc[b % 2, rs]).astype(BF16)
+        if half == 0:
+            hid[:, pl.ds(b * TILE, TILE)] = value
         else:
-            finish(b, acc_g[rs] + gate, acc_u[rs] + up, half)
-
-    for half in range(2):
-        for h in range(HALVES):
-            if half == 0:
-                x_copy(h).wait()
-                w_wait(h)
-            else:
-                x_remote(h).wait_recv()
-            half_step(0, h, half)
-            if half == 1:
-                w_start(h + SLOTS)
-
-    @pl.loop(1, blocks)
-    def _(b):
-        for h in range(HALVES):
-            step = b * HALVES + h
-            slot = lax.rem(step, SLOTS)
-            w_wait(step)
-            lhs = xs[:, pl.ds(h * kd, kd)]
-            gate, up = dot(lhs, gbuf[slot]), dot(lhs, ubuf[slot])
-            if h == 0:
-                acc_g[...] = gate
-                acc_u[...] = up
-            else:
-                finish(b, acc_g[...] + gate, acc_u[...] + up, 2)
-
-            @pl.when(step + SLOTS < steps)
-            def _():
-                w_start(step + SLOTS)
-
-            for k in range(DOWN_SLOTS):
-                @pl.when(step + SLOTS == steps + k)
-                def _():
-                    for c in d_copies(k):
-                        c.start()
+            hout[b] = value
+
+    for h in range(PARTS):
+        arrive(0, h)
+        for j in range(AHEAD + 2 * h, SLOTS if h == PARTS - 1 else min(AHEAD + 2 * h + 2, SLOTS)):
+            start_load(j)
+        multiply(0, h, 1, 0, rows)
+    for h in range(0, PARTS, 2):
+        for i in range(2):
+            x_remote(h + i).wait_recv()
+        multiply(0, h, 2, rows, rows)
+        for i in range(2):
+            start_load(h + i + SLOTS)
+    for b in range(1, blocks):
+        for part_of, count in ((0, PARTS // 2), (PARTS // 2, PARTS // 2)) if b == blocks - 1 else ((0, PARTS),):
+            for h in range(part_of, part_of + count):
+                arrive(b, h)
+            multiply(b, part_of, count, 0, 2 * rows)
+            if part_of == 0:
+                hidden(b - 1, 1)
+                hidden(b - 1, 0)
+            for h in range(part_of, part_of + count):
+                start_load(b * PARTS + h + SLOTS)
+            if part_of == 0:
+                h_copy(b - 1).start()
+    hidden(blocks - 1, 1)
+    h_copy(blocks - 1).start()
+    hidden(blocks - 1, 0)
 
     def compute(k):
         slot = k % DOWN_SLOTS
-        for i, c in enumerate(d_copies(k)):
-            c.wait()
-            if k == 0:
-                ks = pl.ds(i * mine, mine)
-                if i == 1:
-                    for b in range(blocks):
-                        h_copy(b).wait_recv()
-                p = dot(hid[:, ks], dbuf[slot, ks])
-                part[k] = p if i == 0 else part[k] + p
-        if k > 0:
+        if k == 0:
+            early = cols - TILE
+            d_copy(k, 0).wait()
+            d_copy(k, 1).wait()
+            for b in range(blocks - 1):
+                h_copy(b).wait_recv()
+            part[k] = dot(hid[:, pl.ds(0, early)], dbuf[slot, pl.ds(0, early)])
+            h_copy(blocks - 1).wait_recv()
+            part[k] = part[k] + dot(hid[:, pl.ds(early, TILE)], dbuf[slot, pl.ds(early, TILE)])
+        else:
+            for i in range(2):
+                d_copy(k, i).wait()
             part[k] = dot(hid[...], dbuf[slot])
         if k + DOWN_SLOTS < n:
-            for c in d_copies(k + DOWN_SLOTS):
-                c.start()
+            for i in range(2):
+                d_copy(k + DOWN_SLOTS, i).start()
 
     plan = reduce_plan(hops)
     place = [{m: q for q, m in enumerate(p)} for p in plan]
@@ -293,7 +296,7 @@
                     if (hop + 1, r) in gplace[way]:
                         ag_copy(way, hop + 1, r).start()
 
-    for h in range(HALVES):
+    for h in range(PARTS):
         x_remote(h).wait_send()
     for b in range(blocks):
         h_copy(b).wait_send()
@@ -311,8 +314,8 @@
         rows, depth = x.shape
         cols = w_gate.shape[1]
         mine = cols // 2
-        blocks = mine // BLOCK
-        kd = depth // HALVES
+        blocks = mine // TILE
+        kd = depth // PARTS
         chunk = depth // n
         height = rows // PIECES
         messages = len(reduce_plan(n // 2)[0])
@@ -320,28 +323,28 @@
         dma = pltpu.SemaphoreType.DMA
         return pl.pallas_call(
             functools.partial(kernel, n),
-            out_shape=jax.ShapeDtypeStruct((rows, depth), BF16),
+            out_shape=pltpu.VMEM((rows, depth), BF16),
             in_specs=[hbm] * 4,
             out_specs=pl.BlockSpec(memory_space=pltpu.VMEM),
             scratch_shapes=[
                 pltpu.VMEM((2 * rows, depth), BF16),
-                pltpu.VMEM((SLOTS, kd, BLOCK), BF16),
-                pltpu.VMEM((SLOTS, kd, BLOCK), BF16),
-                pltpu.VMEM((2 * rows, BLOCK), F32),
-                pltpu.VMEM((2 * rows, BLOCK), F32),
+                pltpu.VMEM((SLOTS, kd, TILE), BF16),
+                pltpu.VMEM((SLOTS, kd, TILE), BF16),
+                pltpu.VMEM((2, 2 * rows, TILE), F32),
+                pltpu.VMEM((2, 2 * rows, TILE), F32),
                 pltpu.VMEM((rows, cols), BF16),
-                pltpu.VMEM((blocks, rows, BLOCK), BF16),
+                pltpu.VMEM((blocks, rows, TILE), BF16),
                 pltpu.VMEM((DOWN_SLOTS, cols, chunk), BF16),
                 pltpu.VMEM((n, rows, chunk), F32),
                 pltpu.VMEM((2, messages, height, chunk), BF16),
                 pltpu.VMEM((2, messages, height, chunk), BF16),
-                dma((HALVES,)), dma((HALVES,)), dma((HALVES,)),
+                dma((PARTS,)), dma((PARTS,)), dma((PARTS,)),
                 dma((2, SLOTS)), dma((blocks,)), dma((blocks,)),
                 dma((DOWN_SLOTS, 2)),
                 dma((2, messages)), dma((2, messages)), dma((2, messages)), dma((2, messages)),
             ],
             compiler_params=pltpu.CompilerParams(
-                collective_id=0, has_side_effects=True, vmem_limit_bytes=64 * 1024 * 1024 - 65536,
+                collective_id=0, has_side_effects=True, vmem_limit_bytes=56 * 1024 * 1024,
             ),
         )(x, w_gate, w_up, w_down)
 

time: 67.6 us -> 63 us (0.932)
  Pallas kernels: 64.6 us -> 61.7 us
  local copies, waits for them, and re-layouts: 2.85 us -> 1.23 us
    pallas_call x1, Pallas kernels: 64.6 us -> 61.7 us  [step(): pl.pallas_call(functools.partial(kernel, n), out_shape=pltpu.VMEM((rows,...]
    unnamed x1, local copies, waits for them, and re-layouts: 2.85 us -> 1.23 us
where the time goes in v2:
time: 63 us; the launch traced here: 62.9 us
  Pallas kernels  61.7 us (98%)
  local copies, waits for them, and re-layouts  1.23 us (2%)
    pallas_call x1, Pallas kernels, step(): pl.pallas_call(functools.partial(kernel, n), out_shape=pltpu.VMEM((rows,...  61.7 us

profile of v2, /device:TPU:22, one launch (start us, length us, event | category | flops | bytes accessed | tf_op | source)
XLA Modules:
  0.0 62.9 jit_solution(5994901466029913008)
XLA Ops:
  0.0 61.7 %shard_map.46 = bf16[128,7168]{1,0:T(8,128)(2,1)S(1)} custom-call(bf16[128,7168]{1,0:T(8,128)(2,1)} %x_ref.1, bf16[7168,2560]{1,0:T(8,128)(2,1)} %wg_ref.1, bf16[7168,2560]{1,0:T(8,128)(2,1)} %wu_ref.1, bf16[2560,7168]{1,0:T(8,128)(2,1)} %wd_ref.1), custom_call_target="tpu_custom_call" | custom-call | tf_op jit(solution)/shard_map/pallas_call | solution.py:324
  61.7 1.2 %copy.6 = bf16[128,7168]{1,0:T(8,128)(2,1)} copy(bf16[128,7168]{1,0:T(8,128)(2,1)S(1)} %shard_map.46) | data formatting | bytes 3670016

commit v3 on v2

--- a/solution.py
+++ b/solution.py
@@ -13,7 +13,9 @@
 TILE = 256
 PARTS = 4
 SLOTS = 12
-AHEAD = 3
+START = 3
+AHEAD = 5
+EARLY = 1
 DOWN_SLOTS = 4
 PIECES = 4
 
@@ -118,25 +120,23 @@
     loads = [w_copies(s) for s in range(steps)] + [
         (d_copy(k, i),) for k in range(DOWN_SLOTS) for i in range(2)
     ]
-
-    def start_load(j):
-        if j < len(loads):
-            for c in loads[j]:
+    asked, freed = [0], [0]
+
+    def ask(upto):
+        while asked[0] < min(upto, len(loads)) and (asked[0] >= steps or asked[0] < freed[0] + SLOTS):
+            for c in loads[asked[0]]:
                 c.start()
+            asked[0] += 1
 
     for h in range(PARTS):
         x_copy(h).start()
-    for j in range(AHEAD):
-        start_load(j)
+        ask(min(h + 1, START))
 
     barrier = pltpu.get_barrier_semaphore()
     for who in (partner,) + ways:
         pl.semaphore_signal(barrier, inc=1, device_id=who, device_id_type=MESH)
 
     pl.semaphore_wait(barrier, 3)
-    for h in range(PARTS):
-        x_copy(h).wait()
-        x_remote(h).start()
 
     def dot(a, b):
         return jnp.dot(a, b, preferred_element_type=F32)
@@ -161,48 +161,62 @@
         else:
             hout[b] = value
 
-    for h in range(PARTS):
-        arrive(0, h)
-        for j in range(AHEAD + 2 * h, SLOTS if h == PARTS - 1 else min(AHEAD + 2 * h + 2, SLOTS)):
-            start_load(j)
-        multiply(0, h, 1, 0, rows)
-    for h in range(0, PARTS, 2):
-        for i in range(2):
-            x_remote(h + i).wait_recv()
-        multiply(0, h, 2, rows, rows)
-        for i in range(2):
-            start_load(h + i + SLOTS)
-    for b in range(1, blocks):
-        for part_of, count in ((0, PARTS // 2), (PARTS // 2, PARTS // 2)) if b == blocks - 1 else ((0, PARTS),):
-            for h in range(part_of, part_of + count):
-                arrive(b, h)
-            multiply(b, part_of, count, 0, 2 * rows)
-            if part_of == 0:
-                hidden(b - 1, 1)
-                hidden(b - 1, 0)
-            for h in range(part_of, part_of + count):
-                start_load(b * PARTS + h + SLOTS)
-            if part_of == 0:
-                h_copy(b - 1).start()
-    hidden(blocks - 1, 1)
-    h_copy(blocks - 1).start()
-    hidden(blocks - 1, 0)
+    for b in range(EARLY):
+        for h in range(PARTS):
+            if b == 0:
+                x_copy(h).wait()
+                x_remote(h).start()
+            arrive(b, h)
+            ask(b * PARTS + h + 1 + AHEAD)
+            multiply(b, h, 1, 0, rows)
+    half = PARTS // 2
+    for b in range(EARLY):
+        for at in (0, half):
+            if b == 0:
+                for h in range(at, at + half):
+                    x_remote(h).wait_recv()
+                ask(EARLY * PARTS + AHEAD + at + half)
+            multiply(b, at, half, rows, rows)
+        if b > 0:
+            hidden(b - 1, 1)
+            hidden(b - 1, 0)
+        freed[0] += PARTS
+        ask((EARLY + 1) * PARTS + AHEAD)
+        if b > 0:
+            h_copy(b - 1).start()
+    for b in range(EARLY, blocks - 1):
+        for h in range(PARTS):
+            arrive(b, h)
+        ask((b + 1) * PARTS + AHEAD)
+        multiply(b, 0, PARTS, 0, 2 * rows)
+        hidden(b - 1, 1)
+        hidden(b - 1, 0)
+        freed[0] += PARTS
+        ask((b + 2) * PARTS + AHEAD)
+        h_copy(b - 1).start()
+    b = blocks - 1
+    for at in (0, half):
+        for h in range(at, at + half):
+            arrive(b, h)
+        ask(len(loads))
+        multiply(b, at, half, rows, rows)
+        if at == 0:
+            hidden(b - 1, 1)
+            hidden(b - 1, 0)
+            h_copy(b - 1).start()
+    hidden(b, 1)
+    h_copy(b).start()
+    multiply(b, 0, PARTS, 0, rows)
+    hidden(b, 0)
 
     def compute(k):
         slot = k % DOWN_SLOTS
+        for i in range(2):
+            d_copy(k, i).wait()
         if k == 0:
-            early = cols - TILE
-            d_copy(k, 0).wait()
-            d_copy(k, 1).wait()
-            for b in range(blocks - 1):
+            for b in range(blocks):
                 h_copy(b).wait_recv()
-            part[k] = dot(hid[:, pl.ds(0, early)], dbuf[slot, pl.ds(0, early)])
-            h_copy(blocks - 1).wait_recv()
-            part[k] = part[k] + dot(hid[:, pl.ds(early, TILE)], dbuf[slot, pl.ds(early, TILE)])
-        else:
-            for i in range(2):
-                d_copy(k, i).wait()
-            part[k] = dot(hid[...], dbuf[slot])
+        part[k] = dot(hid[...], dbuf[slot])
         if k + DOWN_SLOTS < n:
             for i in range(2):
                 d_copy(k + DOWN_SLOTS, i).start()
@@ -244,16 +258,15 @@
     compute(2)
     for r in SECOND[1][: PIECES // 2]:
         reduce_send(1, 2, r)
-    for k in range(3, min(5, n)):
-        compute(k)
+    compute(3)
     reduce_hop(2, range(PIECES // 2, PIECES))
-    for k in range(5, n - 1):
-        compute(k)
-    if hops > 2:
-        reduce_hop(3, range(PIECES))
-    compute(n - 1)
-    for hop in range(4, hops + 1):
-        reduce_hop(hop, range(PIECES))
+    compute(4)
+    compute(5)
+    reduce_hop(3, range(PIECES // 2))
+    compute(6)
+    reduce_hop(3, range(PIECES // 2, PIECES))
+    compute(7)
+    reduce_hop(4, range(PIECES))
 
     gplan = gather_plan(hops)
     gplace = [{m: q for q, m in enumerate(p)} for p in gplan]

time: 63 us -> 62.6 us (level)
  no operation moved by 1% of the time
where the time goes in v3:
time: 62.6 us; the launch traced here: 62.5 us
  Pallas kernels  61.3 us (98%)
  local copies, waits for them, and re-layouts  1.23 us (2%)
    pallas_call x1, Pallas kernels, step(): pl.pallas_call(functools.partial(kernel, n), out_shape=pltpu.VMEM((rows,...  61.3 us

profile of v3, /device:TPU:22, one launch (start us, length us, event | category | flops | bytes accessed | tf_op | source)
XLA Modules:
  0.0 62.5 jit_solution(8289070586159398054)
XLA Ops:
  0.0 61.3 %shard_map.46 = bf16[128,7168]{1,0:T(8,128)(2,1)S(1)} custom-call(bf16[128,7168]{1,0:T(8,128)(2,1)} %x_ref.1, bf16[7168,2560]{1,0:T(8,128)(2,1)} %wg_ref.1, bf16[7168,2560]{1,0:T(8,128)(2,1)} %wu_ref.1, bf16[2560,7168]{1,0:T(8,128)(2,1)} %wd_ref.1), custom_call_target="tpu_custom_call" | custom-call | tf_op jit(solution)/shard_map/pallas_call | solution.py:337
  61.3 1.2 %copy.6 = bf16[128,7168]{1,0:T(8,128)(2,1)} copy(bf16[128,7168]{1,0:T(8,128)(2,1)S(1)} %shard_map.46) | data formatting | bytes 3670016

commit v4 on v3

--- a/solution.py
+++ b/solution.py
@@ -14,7 +14,7 @@
 PARTS = 4
 SLOTS = 12
 START = 3
-AHEAD = 5
+AHEAD = 7
 EARLY = 1
 DOWN_SLOTS = 4
 PIECES = 4
@@ -185,15 +185,19 @@
         if b > 0:
             h_copy(b - 1).start()
     for b in range(EARLY, blocks - 1):
-        for h in range(PARTS):
-            arrive(b, h)
-        ask((b + 1) * PARTS + AHEAD)
-        multiply(b, 0, PARTS, 0, 2 * rows)
-        hidden(b - 1, 1)
-        hidden(b - 1, 0)
-        freed[0] += PARTS
-        ask((b + 2) * PARTS + AHEAD)
-        h_copy(b - 1).start()
+        for at in (0, half):
+            for h in range(at, at + half):
+                arrive(b, h)
+            ask(b * PARTS + at + half + AHEAD)
+            multiply(b, at, half, 0, 2 * rows)
+            if at == 0:
+                hidden(b - 1, 1)
+                hidden(b - 1, 0)
+            freed[0] += half
+            ask(b * PARTS + at + half + AHEAD)
+            if at == 0:
+                h_copy(b - 1).start()
+
     b = blocks - 1
     for at in (0, half):
         for h in range(at, at + half):

time: 62.6 us -> 62.3 us (level)
  no operation moved by 1% of the time
where the time goes in v4:
time: 62.3 us; the launch traced here: 62.2 us
  Pallas kernels  61 us (98%)
  local copies, waits for them, and re-layouts  1.23 us (2%)
    pallas_call x1, Pallas kernels, step(): pl.pallas_call(functools.partial(kernel, n), out_shape=pltpu.VMEM((rows,...  61 us

profile of v4, /device:TPU:22, one launch (start us, length us, event | category | flops | bytes accessed | tf_op | source)
XLA Modules:
  0.0 62.2 jit_solution(17297495859668622874)
XLA Ops:
  0.0 61.0 %shard_map.46 = bf16[128,7168]{1,0:T(8,128)(2,1)S(1)} custom-call(bf16[128,7168]{1,0:T(8,128)(2,1)} %x_ref.1, bf16[7168,2560]{1,0:T(8,128)(2,1)} %wg_ref.1, bf16[7168,2560]{1,0:T(8,128)(2,1)} %wu_ref.1, bf16[2560,7168]{1,0:T(8,128)(2,1)} %wd_ref.1), custom_call_target="tpu_custom_call" | custom-call | tf_op jit(solution)/shard_map/pallas_call | solution.py:341
  61.0 1.2 %copy.6 = bf16[128,7168]{1,0:T(8,128)(2,1)} copy(bf16[128,7168]{1,0:T(8,128)(2,1)S(1)} %shard_map.46) | data formatting | bytes 3670016

commit v5 on v4

--- a/solution.py
+++ b/solution.py
@@ -305,6 +305,13 @@
         y_ref[rs, own] = total.astype(BF16)
         for way in range(2):
             ag_copy(way, 1, r).start()
+    for h in range(PARTS):
+        x_remote(h).wait_send()
+    for b in range(blocks):
+        h_copy(b).wait_send()
+    for way in range(2):
+        for q in range(len(plan[way])):
+            rs_copy(way, q).wait_send()
     for hop in range(1, hops + 1):
         for r in FINAL:
             for way in range(2):
@@ -313,13 +320,7 @@
                     if (hop + 1, r) in gplace[way]:
                         ag_copy(way, hop + 1, r).start()
 
-    for h in range(PARTS):
-        x_remote(h).wait_send()
-    for b in range(blocks):
-        h_copy(b).wait_send()
     for way in range(2):
-        for q in range(len(plan[way])):
-            rs_copy(way, q).wait_send()
         for hop, r in gplan[way]:
             ag_copy(way, hop, r).wait_send()
 

time: 62.3 us -> 62.2 us (level)
  no operation moved by 1% of the time
where the time goes in v5:
time: 62.2 us
  Pallas kernels  60.9 us (98%)
  local copies, waits for them, and re-layouts  1.23 us (2%)
    pallas_call x1, Pallas kernels, step(): pl.pallas_call(functools.partial(kernel, n), out_shape=pltpu.VMEM((rows,...  60.9 us

profile of v5, /device:TPU:22, one launch (start us, length us, event | category | flops | bytes accessed | tf_op | source)
XLA Modules:
  0.0 62.2 jit_solution(13772374170666491640)
XLA Ops:
  0.0 60.9 %shard_map.46 = bf16[128,7168]{1,0:T(8,128)(2,1)S(1)} custom-call(bf16[128,7168]{1,0:T(8,128)(2,1)} %x_ref.1, bf16[7168,2560]{1,0:T(8,128)(2,1)} %wg_ref.1, bf16[7168,2560]{1,0:T(8,128)(2,1)} %wu_ref.1, bf16[2560,7168]{1,0:T(8,128)(2,1)} %wd_ref.1), custom_call_target="tpu_custom_call" | custom-call | tf_op jit(solution)/shard_map/pallas_call | solution.py:342
  60.9 1.2 %copy.6 = bf16[128,7168]{1,0:T(8,128)(2,1)} copy(bf16[128,7168]{1,0:T(8,128)(2,1)S(1)} %shard_map.46) | data formatting | bytes 3670016
